TPU v7x, 256 devices: a whole 4x4x8 slice. The times are simulated.
256 devices in a mesh: slab: 32 (over x, y, core), probe: 8 (over z).
Axes of the slice: x: 4, y: 4, z: 8, core: 2. Of those that a mesh axis runs over, the one named last changes fastest.
Arguments:
- probes: float32 [16, 3, 64, 128, 128], P('probe', None, 'slab'), may hold values from -50 to 50
- earlier: float32 [16, 3, 64, 128, 128], P(None, None, 'slab', 'probe'), may hold values from -16 to 16
- modulus: float32 [64, 128, 128], P('slab'), may hold values from 0.5 to 2
- tangent: float32 [6, 64, 128, 128], P(None, 'slab'), may hold values from -0.3 to 2, as said below
Outputs:
- basis: float32 [16, 3, 64, 128, 128], P('probe', None, 'slab')
- correlation: float32 [16, 16], replicated
Inputs may be any that keep to these rules, and one draw needn't show every extreme that they name: `tangent`: entries 0 to 2 lie in 1 to 2, entries 3 to 5 in -0.3 to 0.3.
All inputs are finite; a program needn't handle non-finite values.
Results may differ from a plain program's by a relative error of at most 0.00014.
Values sent between devices are 32-bit elements; how exact they have to be, the bound alone decides.
No kernel may reach another device: no remote copies, remote signals or barrier semaphores. Data moves between devices by JAX's collectives and lax.ppermute only.
A program may use at most 64 MiB of HBM per device.

v0:
```python
import jax
import jax.numpy as jnp
from jax import lax
from jax.sharding import PartitionSpec as P


def padded_2(cells, sides, width):
    for axis, dim in sides:
        count = lax.axis_size(axis)
        ends = count - 1
        head = lax.slice_in_dim(cells, 0, width, axis=dim)
        tail = lax.slice_in_dim(cells, cells.shape[dim] - width, cells.shape[dim], axis=dim)
        cells = jnp.concatenate(
            [
                lax.ppermute(tail, axis, [(i, (i + 1) % count) for i in range(ends)]),
                cells,
                lax.ppermute(head, axis, [((i + 1) % count, i) for i in range(ends)]),
            ],
            axis=dim,
        )
    return cells


def scaled_tangent(vectors, modulus, tensor):
    planes = vectors.shape[2] - 2
    height = vectors.shape[3]
    breadth = vectors.shape[4]
    padded = jnp.pad(vectors, ((0, 0), (0, 0), (0, 0), (1, 1), (1, 1)))
    mod_pad = jnp.pad(modulus, ((0, 0), (1, 1), (1, 1)))
    centre = padded[:, :, 1 : planes + 1, 1 : height + 1, 1 : breadth + 1]
    mod_centre = mod_pad[1 : planes + 1, 1 : height + 1, 1 : breadth + 1]
    summed = jnp.zeros_like(centre)
    for step_z in (-1, 0, 1):
        for step_y in (-1, 0, 1):
            for step_x in (-1, 0, 1):
                reach = abs(step_z) + abs(step_y) + abs(step_x)
                if reach == 0:
                    continue
                weight = (0.3, 0.1, 0.05)[reach - 1]
                nearby = padded[
                    :,
                    :,
                    1 + step_z : planes + 1 + step_z,
                    1 + step_y : height + 1 + step_y,
                    1 + step_x : breadth + 1 + step_x,
                ]
                mod_near = mod_pad[
                    1 + step_z : planes + 1 + step_z,
                    1 + step_y : height + 1 + step_y,
                    1 + step_x : breadth + 1 + step_x,
                ]
                edge_coef = 0.5 * weight * (mod_centre + mod_near)
                summed = summed + edge_coef * (centre - nearby)
    first_c = centre[:, 0]
    second_c = centre[:, 1]
    third_c = centre[:, 2]
    local_part = jnp.stack(
        [
            tensor[0] * first_c + tensor[3] * second_c + tensor[4] * third_c,
            tensor[3] * first_c + tensor[1] * second_c + tensor[5] * third_c,
            tensor[4] * first_c + tensor[5] * second_c + tensor[2] * third_c,
        ],
        axis=1,
    )
    return (summed + local_part - 8.0 * centre) / 8.0


def body(probes, earlier, modulus, tangent):
    depth = probes.shape[2]
    slabs = lax.axis_size("slab")
    highest = lax.Precision.HIGHEST
    ext_probe, ext_mod = (
        padded_2(probes, (("slab", 2),), 1),
        padded_2(modulus[None, None], (("slab", 2),), 1),
    )
    mod_wide = ext_mod[0, 0]
    first = scaled_tangent(ext_probe, mod_wide, tangent)
    ext_first = padded_2(first, (("slab", 2),), 1)
    second = scaled_tangent(ext_first, mod_wide, tangent)
    filtered = 2.0 * second - probes
    rows_y = lax.all_to_all(filtered, "probe", split_axis=3, concat_axis=0, tiled=True)
    flat_y = rows_y.reshape(rows_y.shape[0], -1)
    flat_q = earlier.reshape(earlier.shape[0], -1)
    scale = jnp.sqrt(jnp.float32(3 * depth * slabs * probes.shape[3] * probes.shape[4]))
    qq_part = jnp.dot(flat_q, flat_q.T, precision=highest)
    qy_part = jnp.dot(flat_q, flat_y.T, precision=highest)
    gram_earlier, cross = lax.psum((qq_part, qy_part), ("slab", "probe"))
    coeff = jax.scipy.linalg.cho_solve((jnp.linalg.cholesky(gram_earlier), True), cross)
    residue = flat_y - jnp.dot(coeff.T, flat_q, precision=highest)
    group_width = probes.shape[0]
    groups_total = lax.axis_size("probe")
    groups = [residue[k * group_width : (k + 1) * group_width] for k in range(groups_total)]
    for k in range(groups_total):
        own_group = groups[k]
        group_gram = lax.psum(jnp.dot(own_group, own_group.T, precision=highest), ("slab", "probe"))
        own_group = jax.scipy.linalg.solve_triangular(
            jnp.linalg.cholesky(group_gram), own_group, lower=True
        )
        later = groups[k + 1 :]
        if len(later) > 0:
            remaining = jnp.concatenate(later, axis=0)
            along = lax.psum(jnp.dot(remaining, own_group.T, precision=highest), ("slab", "probe"))
            remaining = remaining - jnp.dot(along, own_group, precision=highest)
            later = [remaining[m * group_width : (m + 1) * group_width] for m in range(len(later))]
        groups = groups[:k] + [own_group] + later
    basis_rows = jnp.concatenate(groups, axis=0)
    basis_rows = (basis_rows * scale).reshape(rows_y.shape)
    basis = lax.all_to_all(basis_rows, "probe", split_axis=0, concat_axis=3, tiled=True)
    return (basis, coeff * scale)


def solution(mesh):
    in_specs = (
        P("probe", None, "slab", None, None),
        P(None, None, "slab", "probe", None),
        P("slab", None, None),
        P(None, "slab", None, None),
    )
    out_specs = (P("probe", None, "slab", None, None), P())
    return jax.shard_map(body, mesh=mesh, in_specs=in_specs, out_specs=out_specs, check_vma=False)
```

profile of v0, /device:TPU:2, one launch (start us, length us, event | category | flops | bytes accessed | tf_op | source)
XLA Modules:
  0.0 1344.2 jit_solution(6016094942642158708)
XLA Ops:
  0.7 1.0 fusion.249
  1.6 1.9 collective-permute-start
  3.5 5.8 collective-permute-start.1
  9.3 1.2 fusion.248
  10.5 1.9 collective-permute-start.2
  12.4 5.8 collective-permute-start.3
  18.2 1.3 slice_bitcast_fusion.5
  19.5 1.1 multiply_add_fusion.5
  21.0 1.2 fusion.133
  22.3 1.2 collective-permute-done.3
  23.4 1.5 select_maximum_fusion.2
  24.9 5.1 broadcast_multiply_fusion.1
  30.3 1.9 collective-permute-start.4
  32.2 5.9 collective-permute-start.5
  38.1 2.2 multiply_add_fusion.2
  40.3 1.3 collective-permute-done.4
  41.7 1.8 collective-permute-done.5
  43.4 1.5 select_maximum_fusion
  44.9 5.5 fusion.10
  50.4 1.5 copy.134
  51.9 8.5 all-to-all-start
  60.4 1.4 convolution_bitcast_fusion.2
  61.8 23.6 %all-to-all-done = f32[2,3,2,128,128]{4,1,2,0,3:T(4,128)S(1)} async-done(((f32[2,3,2,128,128]{4,1,2,0,3:T(4,128)}), f32[2,3,2,128,128]{4,1,2,0,3:T(4,128)S(1)}, u32[]{:S(2)}, u32[]{:S(2)}) %all-to-all-start) | async-done | bytes 786464 | tf_op jit(solution)/shard_map/all_to_all | solution.py:81
  85.9 1.4 convolution_bitcast_fusion.1
  87.2 76.8 %all-reduce.3 = (f32[16,16]{0,1:T(8,128)S(1)}, f32[16,16]{0,1:T(8,128)S(1)}) all-reduce(f32[16,16]{0,1:T(8,128)S(1)} %convolution_bitcast_fusion.1, f32[16,16]{0,1:T(8,128)S(1)} %convolution_bitcast_fusion.2), channel_id=1, replica_groups=mesh['slab'=32,'probe'=8] {'slab','probe'}, use_global_device_ids=true, to_apply=%region_3.4 | all-reduce | flops 512 | bytes 4096 | tf_op jit(solution)/shard_map/psum | solution.py:87
  164.1 1.5 cholesky.30
  166.9 1.2 custom-call.15
  168.3 0.8 broadcast_multiply_fusion.2
  169.1 1.2 convolution_subtract_fusion
  170.2 0.9 fusion.214
  171.2 74.2 %psum.121 = f32[2,2]{0,1:T(2,128)S(1)} all-reduce(f32[2,2]{0,1:T(2,128)S(1)} %fusion.214), channel_id=1, replica_groups=mesh['slab'=32,'probe'=8] {'slab','probe'}, use_global_device_ids=true, to_apply=%region_4.5 | all-reduce | flops 4 | bytes 32 | tf_op jit(solution)/shard_map/psum | solution.py:95
  247.8 1.0 fusion.124
  248.8 73.3 %psum.122 = f32[14,2]{0,1:T(2,128)S(1)} all-reduce(f32[14,2]{0,1:T(2,128)S(1)} %fusion.124), channel_id=1, replica_groups=mesh['slab'=32,'probe'=8] {'slab','probe'}, use_global_device_ids=true, to_apply=%region_7.10 | all-reduce | flops 28 | bytes 224 | tf_op jit(solution)/shard_map/psum | solution.py:102
  322.1 0.9 convolution_subtract_fusion.3
  323.0 0.9 fusion.210
  324.0 74.3 %psum.123 = f32[2,2]{0,1:T(2,128)S(1)} all-reduce(f32[2,2]{0,1:T(2,128)S(1)} %fusion.210), channel_id=1, replica_groups=mesh['slab'=32,'probe'=8] {'slab','probe'}, use_global_device_ids=true, to_apply=%region_8.11 | all-reduce | flops 4 | bytes 32 | tf_op jit(solution)/shard_map/psum | solution.py:95
  400.6 1.0 fusion.122
  401.6 73.3 %psum.124 = f32[12,2]{0,1:T(2,128)S(1)} all-reduce(f32[12,2]{0,1:T(2,128)S(1)} %fusion.122), channel_id=1, replica_groups=mesh['slab'=32,'probe'=8] {'slab','probe'}, use_global_device_ids=true, to_apply=%region_9.12 | all-reduce | flops 24 | bytes 192 | tf_op jit(solution)/shard_map/psum | solution.py:102
  475.0 0.9 convolution_subtract_fusion.2
  475.9 0.9 fusion.206
  476.8 74.4 %psum.125 = f32[2,2]{0,1:T(2,128)S(1)} all-reduce(f32[2,2]{0,1:T(2,128)S(1)} %fusion.206), channel_id=1, replica_groups=mesh['slab'=32,'probe'=8] {'slab','probe'}, use_global_device_ids=true, to_apply=%region_10.13 | all-reduce | flops 4 | bytes 32 | tf_op jit(solution)/shard_map/psum | solution.py:95
  553.6 1.0 fusion.120
  554.6 73.3 %psum.126 = f32[10,2]{0,1:T(2,128)S(1)} all-reduce(f32[10,2]{0,1:T(2,128)S(1)} %fusion.120), channel_id=1, replica_groups=mesh['slab'=32,'probe'=8] {'slab','probe'}, use_global_device_ids=true, to_apply=%region_11.14 | all-reduce | flops 20 | bytes 160 | tf_op jit(solution)/shard_map/psum | solution.py:102
  627.9 0.9 convolution_subtract_fusion.1
  628.8 0.9 fusion.202
  629.8 74.2 %psum.127 = f32[2,2]{0,1:T(2,128)S(1)} all-reduce(f32[2,2]{0,1:T(2,128)S(1)} %fusion.202), channel_id=1, replica_groups=mesh['slab'=32,'probe'=8] {'slab','probe'}, use_global_device_ids=true, to_apply=%region_12.15 | all-reduce | flops 4 | bytes 32 | tf_op jit(solution)/shard_map/psum | solution.py:95
  706.4 0.9 fusion.128
  707.3 73.3 %psum.128 = f32[8,2]{0,1:T(2,128)S(1)} all-reduce(f32[8,2]{0,1:T(2,128)S(1)} %fusion.128), channel_id=1, replica_groups=mesh['slab'=32,'probe'=8] {'slab','probe'}, use_global_device_ids=true, to_apply=%region_13.16 | all-reduce | flops 16 | bytes 128 | tf_op jit(solution)/shard_map/psum | solution.py:102
  781.2 0.9 fusion.198
  782.2 74.2 %psum.129 = f32[2,2]{0,1:T(2,128)S(1)} all-reduce(f32[2,2]{0,1:T(2,128)S(1)} %fusion.198), channel_id=1, replica_groups=mesh['slab'=32,'probe'=8] {'slab','probe'}, use_global_device_ids=true, to_apply=%region_14.17 | all-reduce | flops 4 | bytes 32 | tf_op jit(solution)/shard_map/psum | solution.py:95
  858.8 0.9 fusion.126
  859.7 73.3 %psum.130 = f32[6,2]{0,1:T(2,128)S(1)} all-reduce(f32[6,2]{0,1:T(2,128)S(1)} %fusion.126), channel_id=1, replica_groups=mesh['slab'=32,'probe'=8] {'slab','probe'}, use_global_device_ids=true, to_apply=%region_15.18 | all-reduce | flops 12 | bytes 96 | tf_op jit(solution)/shard_map/psum | solution.py:102
  933.6 0.9 fusion.194
  934.5 74.4 %psum.131 = f32[2,2]{0,1:T(2,128)S(1)} all-reduce(f32[2,2]{0,1:T(2,128)S(1)} %fusion.194), channel_id=1, replica_groups=mesh['slab'=32,'probe'=8] {'slab','probe'}, use_global_device_ids=true, to_apply=%region_16.19 | all-reduce | flops 4 | bytes 32 | tf_op jit(solution)/shard_map/psum | solution.py:95
  1011.4 0.9 fusion.130
  1012.3 73.3 %psum.132 = f32[4,2]{0,1:T(2,128)S(1)} all-reduce(f32[4,2]{0,1:T(2,128)S(1)} %fusion.130), channel_id=1, replica_groups=mesh['slab'=32,'probe'=8] {'slab','probe'}, use_global_device_ids=true, to_apply=%region_17.20 | all-reduce | flops 8 | bytes 64 | tf_op jit(solution)/shard_map/psum | solution.py:102
  1086.2 0.9 fusion.190
  1087.1 74.2 %psum.133 = f32[2,2]{0,1:T(2,128)S(1)} all-reduce(f32[2,2]{0,1:T(2,128)S(1)} %fusion.190), channel_id=1, replica_groups=mesh['slab'=32,'probe'=8] {'slab','probe'}, use_global_device_ids=true, to_apply=%region_18.21 | all-reduce | flops 4 | bytes 32 | tf_op jit(solution)/shard_map/psum | solution.py:95
  1163.7 0.9 fusion.186
  1164.7 73.3 %psum.134 = f32[2,2]{1,0:T(2,128)S(1)} all-reduce(f32[2,2]{1,0:T(2,128)S(1)} %fusion.186), channel_id=1, replica_groups=mesh['slab'=32,'probe'=8] {'slab','probe'}, use_global_device_ids=true, to_apply=%region_19.22 | all-reduce | flops 4 | bytes 32 | tf_op jit(solution)/shard_map/psum | solution.py:102
  1238.5 0.9 fusion.250
  1239.4 74.2 %psum.135 = f32[2,2]{0,1:T(2,128)S(1)} all-reduce(f32[2,2]{0,1:T(2,128)S(1)} %fusion.250), channel_id=1, replica_groups=mesh['slab'=32,'probe'=8] {'slab','probe'}, use_global_device_ids=true, to_apply=%region_20.23 | all-reduce | flops 4 | bytes 32 | tf_op jit(solution)/shard_map/psum | solution.py:95
  1316.4 26.6 %all_to_all.33 = f32[16,3,2,16,128]{4,3,2,1,0:T(8,128)S(1)} all-to-all(f32[16,3,2,16,128]{4,3,2,1,0:T(8,128)S(1)} %broadcast_multiply_fusion), channel_id=1, replica_groups=mesh['slab'=32,'probe'=8] {'probe'}, dimensions={0} | all-to-all | bytes 1572864 | tf_op jit(solution)/shard_map/all_to_all | solution.py:108
  1343.0 0.9 copy.164
  (153 shorter events, 23.7 us)
Async XLA Ops:
  0.6 20.0 %copy-start.2 = (f32[2,128,128]{2,1,0:T(8,128)S(1)}, f32[2,128,128]{2,1,0:T(8,128)}, u32[]{:S(2)}) copy-start(f32[2,128,128]{2,1,0:T(8,128)} %param.9) | copy-start | bytes 393220
  0.6 18.9 %copy-start = (f32[2,3,2,128,128]{4,3,2,1,0:T(8,128)S(1)}, f32[2,3,2,128,128]{4,3,2,1,0:T(8,128)}, u32[]{:S(2)}) copy-start(f32[2,3,2,128,128]{4,3,2,1,0:T(8,128)} %param.7) | copy-start | bytes 2359300
  1.6 19.0 %collective-permute-start = (f32[1,1,1,128,128]{4,3,2,1,0:T(8,128)S(1)}, f32[1,1,1,128,128]{4,3,2,1,0:T(8,128)S(1)}, u32[]{:S(2)}, u32[]{:S(2)}) collective-permute-start(f32[1,1,1,128,128]{4,3,2,1,0:T(8,128)S(1)} %get-tuple-element.52), channel_id=1, source_target_pairs={{0,8},{8,16},{16,24},{24,32},{32,40},{40,48},{48,56},{56,64},{64,7... | collective-permute-start | bytes 196616 | tf_op jit(solution)/shard_map/ppermute | solution.py:15
  3.5 17.1 %collective-permute-start.1 = (f32[1,1,1,128,128]{4,3,2,1,0:T(8,128)S(1)}, f32[1,1,1,128,128]{4,3,2,1,0:T(8,128)S(1)}, u32[]{:S(2)}, u32[]{:S(2)}) collective-permute-start(f32[1,1,1,128,128]{4,3,2,1,0:T(8,128)S(1)} %get-tuple-element.53), channel_id=1, source_target_pairs={{8,0},{16,8},{24,16},{32,24},{40,32},{48,40},{56,48},{64,56},{72,6... | collective-permute-start | bytes 196616 | tf_op jit(solution)/shard_map/ppermute | solution.py:17
  10.5 11.8 collective-permute-start.2
  12.4 11.0 collective-permute-start.3
  19.4 1.2 copy-start.21
  19.4 1.2 copy-start.22
  19.5 1.2 copy-start.23
  19.5 1.2 copy-start.24
  19.5 1.2 copy-start.25
  19.5 1.2 copy-start.26
  21.0 9.1 copy-start.3
  22.1 7.9 copy-start.4
  22.1 7.9 copy-start.5
  22.1 7.9 copy-start.6
  22.1 7.9 copy-start.7
  22.1 7.9 copy-start.8
  22.1 7.9 copy-start.9
  22.2 7.9 copy-start.10
  22.2 7.9 copy-start.11
  22.2 7.9 copy-start.12
  22.2 7.9 copy-start.13
  22.2 7.9 copy-start.14
  22.2 7.9 copy-start.15
  22.2 7.9 copy-start.16
  22.2 7.9 copy-start.17
  22.2 7.9 copy-start.18
  22.2 7.9 copy-start.19
  22.3 7.9 copy-start.20
  30.3 11.4 collective-permute-start.4
  32.2 11.2 collective-permute-start.5
  50.4 10.0 copy-start.1
  51.9 33.5 %all-to-all-start = ((f32[2,3,2,128,128]{4,1,2,0,3:T(4,128)}), f32[2,3,2,128,128]{4,1,2,0,3:T(4,128)S(1)}, u32[]{:S(2)}, u32[]{:S(2)}) async-start(f32[2,3,2,128,128]{4,1,2,0,3:T(4,128)} %copy.134), calls=%async_computation | async-start | bytes 2097152 | tf_op jit(solution)/shard_map/all_to_all | solution.py:81
where the time goes:
time: 1360 us; the launch traced here: 1340 us
  blocking collectives  1210 us (89%)
  other arithmetic  36 us (3%)
  starting transfers between devices  31.7 us (2%)
  matrix products  28.7 us (2%)
  waiting for transfers between devices  27.9 us (2%)
    psum x8, blocking collectives, body(): lax.psum(jnp.dot(own_group, own_group.T, precision=highest), ('slab', 'pr...  594 us
    psum x7, blocking collectives, body(): lax.psum(jnp.dot(remaining, own_group.T, precision=highest), ('slab', 'pr...  513 us
    psum x1, blocking collectives, body(): gram_earlier, cross = lax.psum((qq_part, qy_part), ('slab', 'probe'))  76.8 us
  transfers between devices with their start and end apart: 7, of which 4 were waited for; matrix products, arithmetic and copies ran while one was open for 1% of the time, Pallas kernels for 0%

commit v1 on v0

--- a/solution.py
+++ b/solution.py
@@ -99,7 +99,9 @@
         later = groups[k + 1 :]
         if len(later) > 0:
             remaining = jnp.concatenate(later, axis=0)
-            along = lax.psum(jnp.dot(remaining, own_group.T, precision=highest), ("slab", "probe"))
+            x = jnp.dot(remaining, own_group.T, precision=highest)
+            parts = lax.all_gather(x, ("slab", "probe"))
+            along = jnp.sum(parts, axis=0)
             remaining = remaining - jnp.dot(along, own_group, precision=highest)
             later = [remaining[m * group_width : (m + 1) * group_width] for m in range(len(later))]
         groups = groups[:k] + [own_group] + later

time: 1360 us -> 1270 us (0.934)
  blocking collectives: 1210 us -> 1120 us
    psum x7 -> x0, blocking collectives: 513 us -> none  [body(): lax.psum(jnp.dot(remaining, own_group.T, precision=highest), ('slab', 'pr...]
    all_gather x0 -> x7, blocking collectives: none -> 440 us  [body(): parts = lax.all_gather(x, ('slab', 'probe'))]
where the time goes in v1:
time: 1270 us; the launch traced here: 1260 us
  blocking collectives  1120 us (88%)
  other arithmetic  37.9 us (3%)
  starting transfers between devices  31.7 us (2%)
  matrix products  28.7 us (2%)
  waiting for transfers between devices  27.9 us (2%)
    psum x8, blocking collectives, body(): lax.psum(jnp.dot(own_group, own_group.T, precision=highest), ('slab', 'pr...  581 us
    all_gather x7, blocking collectives, body(): parts = lax.all_gather(x, ('slab', 'probe'))  440 us
    psum x1, blocking collectives, body(): gram_earlier, cross = lax.psum((qq_part, qy_part), ('slab', 'probe'))  76.8 us
    all_to_all x1, blocking collectives, body(): lax.all_to_all(basis_rows, 'probe', split_axis=0, concat_axis=3, tiled=True)  26.5 us
  transfers between devices with their start and end apart: 7, of which 4 were waited for; matrix products, arithmetic and copies ran while one was open for 1% of the time, Pallas kernels for 0%

profile of v1, /device:TPU:2, one launch (start us, length us, event | category | flops | bytes accessed | tf_op | source)
XLA Modules:
  0.0 1259.8 jit_solution(4784023116080931405)
XLA Ops:
  0.7 1.0 fusion.242
  1.6 1.9 collective-permute-start
  3.5 5.8 collective-permute-start.1
  9.3 1.2 fusion.241
  10.5 1.9 collective-permute-start.2
  12.4 5.8 collective-permute-start.3
  18.2 1.3 slice_bitcast_fusion.5
  19.5 1.1 multiply_add_fusion.5
  21.0 1.2 fusion.127
  22.3 1.2 collective-permute-done.3
  23.4 1.5 select_maximum_fusion.2
  24.9 5.1 broadcast_multiply_fusion.1
  30.3 1.9 collective-permute-start.4
  32.2 5.9 collective-permute-start.5
  38.1 2.2 multiply_add_fusion.2
  40.3 1.3 collective-permute-done.4
  41.7 1.8 collective-permute-done.5
  43.4 1.5 select_maximum_fusion
  44.9 5.5 fusion.10
  50.4 1.5 copy.134
  51.9 8.5 all-to-all-start
  60.4 1.4 convolution_bitcast_fusion.2
  61.8 23.6 %all-to-all-done = f32[2,3,2,128,128]{4,1,2,0,3:T(4,128)S(1)} async-done(((f32[2,3,2,128,128]{4,1,2,0,3:T(4,128)}), f32[2,3,2,128,128]{4,1,2,0,3:T(4,128)S(1)}, u32[]{:S(2)}, u32[]{:S(2)}) %all-to-all-start) | async-done | bytes 786464 | tf_op jit(solution)/shard_map/all_to_all | solution.py:81
  85.9 1.4 convolution_bitcast_fusion.1
  87.2 76.8 %all-reduce.3 = (f32[16,16]{0,1:T(8,128)S(1)}, f32[16,16]{0,1:T(8,128)S(1)}) all-reduce(f32[16,16]{0,1:T(8,128)S(1)} %convolution_bitcast_fusion.1, f32[16,16]{0,1:T(8,128)S(1)} %convolution_bitcast_fusion.2), channel_id=1, replica_groups=mesh['slab'=32,'probe'=8] {'slab','probe'}, use_global_device_ids=true, to_apply=%region_3.4 | all-reduce | flops 512 | bytes 4096 | tf_op jit(solution)/shard_map/psum | solution.py:87
  164.1 1.5 cholesky.30
  166.9 1.2 custom-call.15
  168.3 0.8 broadcast_multiply_fusion.2
  169.1 1.2 convolution_subtract_fusion
  170.2 0.9 fusion.207
  171.2 74.2 %psum.72 = f32[2,2]{0,1:T(2,128)S(1)} all-reduce(f32[2,2]{0,1:T(2,128)S(1)} %fusion.207), channel_id=1, replica_groups=mesh['slab'=32,'probe'=8] {'slab','probe'}, use_global_device_ids=true, to_apply=%region_4.5 | all-reduce | flops 4 | bytes 32 | tf_op jit(solution)/shard_map/psum | solution.py:95
  247.8 1.0 convolution_bitcast_fusion.5
  248.8 61.7 %all-gather.7 = f32[256,14,2]{1,2,0:T(2,128)S(1)} all-gather(f32[1,14,2]{1,2,0:T(2,128)S(1)} %convolution_bitcast_fusion.5), channel_id=2, replica_groups=mesh['slab'=32,'probe'=8] {'slab','probe'}, dimensions={0}, use_global_device_ids=true | all-gather | bytes 28784 | tf_op jit(solution)/shard_map/all_gather | solution.py:103
  310.8 0.9 convolution_subtract_fusion.3
  311.7 0.9 fusion.203
  312.7 73.3 %psum.73 = f32[2,2]{0,1:T(2,128)S(1)} all-reduce(f32[2,2]{0,1:T(2,128)S(1)} %fusion.203), channel_id=1, replica_groups=mesh['slab'=32,'probe'=8] {'slab','probe'}, use_global_device_ids=true, to_apply=%region_8.11 | all-reduce | flops 4 | bytes 32 | tf_op jit(solution)/shard_map/psum | solution.py:95
  388.3 1.0 convolution_bitcast_fusion.4
  389.4 62.0 %all-gather.8 = f32[256,12,2]{1,2,0:T(2,128)S(1)} all-gather(f32[1,12,2]{1,2,0:T(2,128)S(1)} %convolution_bitcast_fusion.4), channel_id=3, replica_groups=mesh['slab'=32,'probe'=8] {'slab','probe'}, dimensions={0}, use_global_device_ids=true | all-gather | bytes 24672 | tf_op jit(solution)/shard_map/all_gather | solution.py:103
  451.7 0.9 convolution_subtract_fusion.2
  452.6 0.9 fusion.199
  453.5 73.2 %psum.74 = f32[2,2]{0,1:T(2,128)S(1)} all-reduce(f32[2,2]{0,1:T(2,128)S(1)} %fusion.199), channel_id=1, replica_groups=mesh['slab'=32,'probe'=8] {'slab','probe'}, use_global_device_ids=true, to_apply=%region_10.13 | all-reduce | flops 4 | bytes 32 | tf_op jit(solution)/shard_map/psum | solution.py:95
  529.1 1.0 convolution_bitcast_fusion.3
  530.1 62.3 %all-gather.9 = f32[256,10,2]{1,2,0:T(2,128)S(1)} all-gather(f32[1,10,2]{1,2,0:T(2,128)S(1)} %convolution_bitcast_fusion.3), channel_id=4, replica_groups=mesh['slab'=32,'probe'=8] {'slab','probe'}, dimensions={0}, use_global_device_ids=true | all-gather | bytes 20560 | tf_op jit(solution)/shard_map/all_gather | solution.py:103
  592.7 0.9 convolution_subtract_fusion.1
  593.6 0.9 fusion.195
  594.5 72.7 %psum.75 = f32[2,2]{0,1:T(2,128)S(1)} all-reduce(f32[2,2]{0,1:T(2,128)S(1)} %fusion.195), channel_id=1, replica_groups=mesh['slab'=32,'probe'=8] {'slab','probe'}, use_global_device_ids=true, to_apply=%region_12.15 | all-reduce | flops 4 | bytes 32 | tf_op jit(solution)/shard_map/psum | solution.py:95
  669.6 0.9 convolution_bitcast_fusion.9
  670.6 63.0 %all-gather.10 = f32[256,8,2]{1,2,0:T(2,128)S(1)} all-gather(f32[1,8,2]{1,2,0:T(2,128)S(1)} %convolution_bitcast_fusion.9), channel_id=5, replica_groups=mesh['slab'=32,'probe'=8] {'slab','probe'}, dimensions={0}, use_global_device_ids=true | all-gather | bytes 16448 | tf_op jit(solution)/shard_map/all_gather | solution.py:103
  734.4 0.9 fusion.191
  735.3 72.0 %psum.76 = f32[2,2]{0,1:T(2,128)S(1)} all-reduce(f32[2,2]{0,1:T(2,128)S(1)} %fusion.191), channel_id=1, replica_groups=mesh['slab'=32,'probe'=8] {'slab','probe'}, use_global_device_ids=true, to_apply=%region_14.17 | all-reduce | flops 4 | bytes 32 | tf_op jit(solution)/shard_map/psum | solution.py:95
  809.7 0.9 convolution_bitcast_fusion.8
  810.7 63.5 %all-gather.11 = f32[256,6,2]{1,2,0:T(2,128)S(1)} all-gather(f32[1,6,2]{1,2,0:T(2,128)S(1)} %convolution_bitcast_fusion.8), channel_id=6, replica_groups=mesh['slab'=32,'probe'=8] {'slab','probe'}, dimensions={0}, use_global_device_ids=true | all-gather | bytes 12336 | tf_op jit(solution)/shard_map/all_gather | solution.py:103
  875.0 0.9 fusion.187
  876.0 72.0 %psum.77 = f32[2,2]{0,1:T(2,128)S(1)} all-reduce(f32[2,2]{0,1:T(2,128)S(1)} %fusion.187), channel_id=1, replica_groups=mesh['slab'=32,'probe'=8] {'slab','probe'}, use_global_device_ids=true, to_apply=%region_16.19 | all-reduce | flops 4 | bytes 32 | tf_op jit(solution)/shard_map/psum | solution.py:95
  950.3 0.9 convolution_bitcast_fusion.7
  951.3 63.7 %all-gather.12 = f32[256,4,2]{1,2,0:T(2,128)S(1)} all-gather(f32[1,4,2]{1,2,0:T(2,128)S(1)} %convolution_bitcast_fusion.7), channel_id=7, replica_groups=mesh['slab'=32,'probe'=8] {'slab','probe'}, dimensions={0}, use_global_device_ids=true | all-gather | bytes 8224 | tf_op jit(solution)/shard_map/all_gather | solution.py:103
  1015.8 0.9 fusion.183
  1016.7 71.8 %psum.78 = f32[2,2]{0,1:T(2,128)S(1)} all-reduce(f32[2,2]{0,1:T(2,128)S(1)} %fusion.183), channel_id=1, replica_groups=mesh['slab'=32,'probe'=8] {'slab','probe'}, use_global_device_ids=true, to_apply=%region_18.21 | all-reduce | flops 4 | bytes 32 | tf_op jit(solution)/shard_map/psum | solution.py:95
  1090.9 0.9 convolution_bitcast_fusion.6
  1091.9 64.0 %all-gather.13 = f32[256,2,2]{2,1,0:T(2,128)S(1)} all-gather(f32[1,2,2]{2,1,0:T(2,128)S(1)} %convolution_bitcast_fusion.6), channel_id=8, replica_groups=mesh['slab'=32,'probe'=8] {'slab','probe'}, dimensions={0}, use_global_device_ids=true | all-gather | bytes 4112 | tf_op jit(solution)/shard_map/all_gather | solution.py:103
  1156.6 0.9 fusion.243
  1157.6 71.8 %psum.79 = f32[2,2]{0,1:T(2,128)S(1)} all-reduce(f32[2,2]{0,1:T(2,128)S(1)} %fusion.243), channel_id=1, replica_groups=mesh['slab'=32,'probe'=8] {'slab','probe'}, use_global_device_ids=true, to_apply=%region_20.23 | all-reduce | flops 4 | bytes 32 | tf_op jit(solution)/shard_map/psum | solution.py:95
  1232.1 26.5 %all_to_all.33 = f32[16,3,2,16,128]{4,3,2,1,0:T(8,128)S(1)} all-to-all(f32[16,3,2,16,128]{4,3,2,1,0:T(8,128)S(1)} %broadcast_multiply_fusion), channel_id=1, replica_groups=mesh['slab'=32,'probe'=8] {'probe'}, dimensions={0} | all-to-all | bytes 1572864 | tf_op jit(solution)/shard_map/all_to_all | solution.py:110
  1258.7 0.9 copy.164
  (160 shorter events, 25.7 us)
Async XLA Ops:
  0.6 20.0 %copy-start.2 = (f32[2,128,128]{2,1,0:T(8,128)S(1)}, f32[2,128,128]{2,1,0:T(8,128)}, u32[]{:S(2)}) copy-start(f32[2,128,128]{2,1,0:T(8,128)} %param.9) | copy-start | bytes 393220
  0.6 18.9 %copy-start = (f32[2,3,2,128,128]{4,3,2,1,0:T(8,128)S(1)}, f32[2,3,2,128,128]{4,3,2,1,0:T(8,128)}, u32[]{:S(2)}) copy-start(f32[2,3,2,128,128]{4,3,2,1,0:T(8,128)} %param.7) | copy-start | bytes 2359300
  1.6 19.0 %collective-permute-start = (f32[1,1,1,128,128]{4,3,2,1,0:T(8,128)S(1)}, f32[1,1,1,128,128]{4,3,2,1,0:T(8,128)S(1)}, u32[]{:S(2)}, u32[]{:S(2)}) collective-permute-start(f32[1,1,1,128,128]{4,3,2,1,0:T(8,128)S(1)} %get-tuple-element.52), channel_id=1, source_target_pairs={{0,8},{8,16},{16,24},{24,32},{32,40},{40,48},{48,56},{56,64},{64,7... | collective-permute-start | bytes 196616 | tf_op jit(solution)/shard_map/ppermute | solution.py:15
  3.5 17.1 %collective-permute-start.1 = (f32[1,1,1,128,128]{4,3,2,1,0:T(8,128)S(1)}, f32[1,1,1,128,128]{4,3,2,1,0:T(8,128)S(1)}, u32[]{:S(2)}, u32[]{:S(2)}) collective-permute-start(f32[1,1,1,128,128]{4,3,2,1,0:T(8,128)S(1)} %get-tuple-element.53), channel_id=1, source_target_pairs={{8,0},{16,8},{24,16},{32,24},{40,32},{48,40},{56,48},{64,56},{72,6... | collective-permute-start | bytes 196616 | tf_op jit(solution)/shard_map/ppermute | solution.py:17
  10.5 11.8 collective-permute-start.2
  12.4 11.0 collective-permute-start.3
  19.4 1.2 copy-start.21
  19.4 1.2 copy-start.22
  19.5 1.2 copy-start.23
  19.5 1.2 copy-start.24
  19.5 1.2 copy-start.25
  19.5 1.2 copy-start.26
  21.0 9.1 copy-start.3
  22.1 7.9 copy-start.4
  22.1 7.9 copy-start.5
  22.1 7.9 copy-start.6
  22.1 7.9 copy-start.7
  22.1 7.9 copy-start.8
  22.1 7.9 copy-start.9
  22.2 7.9 copy-start.10
  22.2 7.9 copy-start.11
  22.2 7.9 copy-start.12
  22.2 7.9 copy-start.13
  22.2 7.9 copy-start.14
  22.2 7.9 copy-start.15
  22.2 7.9 copy-start.16
  22.2 7.9 copy-start.17
  22.2 7.9 copy-start.18
  22.2 7.9 copy-start.19
  22.3 7.9 copy-start.20
  30.3 11.4 collective-permute-start.4
  32.2 11.2 collective-permute-start.5
  50.4 10.0 copy-start.1
  51.9 33.5 %all-to-all-start = ((f32[2,3,2,128,128]{4,1,2,0,3:T(4,128)}), f32[2,3,2,128,128]{4,1,2,0,3:T(4,128)S(1)}, u32[]{:S(2)}, u32[]{:S(2)}) async-start(f32[2,3,2,128,128]{4,1,2,0,3:T(4,128)} %copy.134), calls=%async_computation | async-start | bytes 2097152 | tf_op jit(solution)/shard_map/all_to_all | solution.py:81
